TPU v7x, 512 devices: a whole 4x4x16 slice. The times are simulated.
512 devices in a mesh: ep: 128 (over x, z, core), dp: 4 (over y).
Axes of the slice: x: 4, y: 4, z: 16, core: 2. Of those that a mesh axis runs over, the one named last changes fastest.
Arguments:
- tokens: bfloat16 [2048, 3584], P('ep'), may hold values from -6 to 6
- expert_ids: int32 [2048, 8], P('ep'), may hold values from 0 to 127, all different within a row; in each aligned block of 16 rows (0 to 15, 16 to 31, ...) at most 4 rows name the same one
- route_logits: float32 [2048, 8], P('ep'), may hold values from -8 to 8
- expert_gate: bfloat16 [128, 3584, 1024], P('ep', None, 'dp'), may hold values from -0.09375 to 0.09375
- expert_up: bfloat16 [128, 3584, 1024], P('ep', None, 'dp'), may hold values from -0.09375 to 0.09375
- expert_down: bfloat16 [128, 1024, 3584], P('ep', 'dp'), may hold values from -0.1875 to 0.1875
Outputs:
- mixed: bfloat16 [2048, 3584], P(('ep', 'dp'))
Inputs may be any that keep to these rules, and one draw needn't show every extreme that they name: `expert_ids`: each row names 8 different experts of 0 to 127 and every expert is named by some row. Within the rows of one index of ep (aligned blocks of 16 rows) no expert is named more than 4 times, and some block names one expert exactly 4 times. Loads are heavy-tailed: a few experts take several times the mean.
All inputs are finite; a program needn't handle non-finite values.
Results may differ from a plain program's by a relative error of at most 0.015.
Values may be sent and summed in bfloat16 or wider, within the bound.
A program may use at most 64 MiB of HBM per device.

v0:
```python
import functools

import jax
import jax.numpy as jnp
from jax import lax
from jax.experimental import pallas as pl
from jax.experimental.pallas import tpu as pltpu
from jax.sharding import PartitionSpec as P

route_scale = 2.5


def by_slots(tokens, expert_ids, route_logits, expert_gate, expert_up, expert_down):
    tok_rows, width = tokens.shape
    top = expert_ids.shape[1]
    n_ep = lax.axis_size("ep")
    n_dp = lax.axis_size("dp")
    experts = n_ep
    capacity = min(tok_rows, 4 * max(1, tok_rows * top // experts))
    flat_ids = expert_ids.reshape(-1).astype(jnp.int32)
    onehot = (flat_ids[:, None] == jnp.arange(experts, dtype=jnp.int32)[None, :]).astype(jnp.int32)
    earlier = jnp.cumsum(onehot, axis=0).astype(jnp.int32) - onehot
    within = jnp.sum(earlier * onehot, axis=1).astype(jnp.int32)
    slot_index = flat_ids * capacity + within
    token_of_slot = jnp.arange(tok_rows * top, dtype=jnp.int32) // top
    source_row = (
        jnp.full((experts * capacity,), tok_rows, jnp.int32).at[slot_index].set(token_of_slot)
    )
    extended = jnp.concatenate([tokens, jnp.zeros((1, width), tokens.dtype)], axis=0)
    outgoing = extended[source_row].reshape(n_ep, capacity, width)
    arrived = lax.all_to_all(outgoing, "ep", split_axis=0, concat_axis=0, tiled=True)
    received = arrived.reshape(n_ep * capacity, width)
    gate = jnp.dot(received, expert_gate[0], preferred_element_type=jnp.float32)
    upper = jnp.dot(received, expert_up[0], preferred_element_type=jnp.float32)
    hidden = (jax.nn.silu(gate) * upper).astype(jnp.bfloat16)
    partial_value = jnp.dot(hidden, expert_down[0], preferred_element_type=jnp.float32)
    partial_value = partial_value.reshape(n_ep, capacity, width)
    scores = jax.nn.sigmoid(route_logits)
    weights = route_scale * scores / jnp.sum(scores, axis=1, keepdims=True)
    member = lax.axis_index("dp")
    quarter = capacity // n_dp
    reduced = (
        lax.psum_scatter(partial_value.astype(jnp.bfloat16), "dp", scatter_dimension=1, tiled=True)
        .astype(jnp.float32)
        .astype(jnp.bfloat16)
    )
    back = lax.all_to_all(reduced, "ep", split_axis=0, concat_axis=0, tiled=True)
    offset = within - member * quarter
    held = ((offset >= 0) & (offset < quarter)).astype(jnp.float32)
    picked = flat_ids * quarter + jnp.clip(offset, 0, quarter - 1)
    values = back.reshape(experts * quarter, width)[picked].reshape(tok_rows, top, width)
    masked = weights * held.reshape(tok_rows, top)
    contrib = jnp.sum(masked[:, :, None] * values.astype(jnp.float32), axis=1)
    routed = lax.psum_scatter(
        contrib.astype(jnp.bfloat16), "dp", scatter_dimension=0, tiled=True
    ).astype(jnp.float32)
    return routed.astype(jnp.bfloat16)


MESH = pl.DeviceIdType.MESH
LANES = 128
RIGHT, LEFT, ACROSS, SIDE, CORE = range(5)


def exchange_kernel(
    planes, tokens_ref, ids_ref, logits_ref, gate_hbm, up_hbm, down_hbm, out_ref,
    tok, w_gate, w_up, w_down, hid, wcol, theirs, part, from_core, from_first, line_out, line_in,
    last_out, last_in,
    weight_sem, tok_send, tok_recv, core_send, core_recv, first_send, first_recv,
    line_send, line_recv, last_send, last_recv,
):
    rows, width = tokens_ref.shape
    top = ids_ref.shape[1]
    hidden = gate_hbm.shape[2]
    wide = tok.shape[1]
    half = wide // 2
    sub = rows // 2
    me, y = lax.axis_index("ep"), lax.axis_index("dp")
    c, x, z = me % 2, (me // 2) % 2, me // 4

    def ep_of(zz, xx, cc):
        return (zz * 2 + xx) * 2 + cc

    def device(kind):
        if kind == RIGHT:
            return (ep_of(z + 1, x, c), y)
        if kind == LEFT:
            return (ep_of(z - 1, x, c), y)
        if kind == ACROSS:
            return (ep_of(z, 1 - x, c), y)
        if kind == SIDE:
            return (me, 1 - y)
        return (ep_of(z, x, 1 - c), y)

    loads = [
        pltpu.make_async_copy(src.at[0], dst, weight_sem.at[i])
        for i, (src, dst) in enumerate(((gate_hbm, w_gate), (up_hbm, w_up), (down_hbm, w_down)))
    ]
    for load in loads:
        load.start()

    barrier = pltpu.get_barrier_semaphore()

    def greet(kind):
        pl.semaphore_signal(barrier, inc=1, device_id=device(kind), device_id_type=MESH)

    for kind in (ACROSS, SIDE, CORE):
        greet(kind)
    pl.when(z > 0)(lambda: greet(LEFT))
    pl.when(z < planes - 1)(lambda: greet(RIGHT))

    scores = jax.nn.sigmoid(logits_ref[...])
    weights = route_scale * scores / jnp.sum(scores, axis=1, keepdims=True)
    lane = lax.broadcasted_iota(jnp.int32, (rows, LANES), 1)
    dense = jnp.zeros((rows, LANES), jnp.float32)
    for k in range(top):
        dense = dense + jnp.where(lane == ids_ref[:, k : k + 1], weights[:, k : k + 1], 0.0)
    coarse = dense.astype(jnp.bfloat16)
    fine = (dense - coarse.astype(jnp.float32)).astype(jnp.bfloat16)
    own_rows = pl.ds(pl.multiple_of(me * rows, rows), rows)
    tok[own_rows, :width] = tokens_ref[...]
    tok[own_rows, width : width + LANES] = coarse
    tok[own_rows, width + LANES :] = fine

    middle = jnp.where(z > 0, 1, 0) + jnp.where(z < planes - 1, 1, 0)
    pl.semaphore_wait(barrier, 3 + middle)

    def unit(block, h):
        return tok.at[
            pl.ds(pl.multiple_of(block * rows, rows), rows),
            pl.ds(pl.multiple_of(h * half, LANES), half),
        ]

    def token_copy(kind, block, h):
        return pltpu.make_async_remote_copy(
            src_ref=unit(block, h),
            dst_ref=unit(block, h),
            send_sem=tok_send.at[kind, block, h],
            recv_sem=tok_recv.at[block, h],
            device_id=device(kind),
            device_id_type=MESH,
        )

    def on_line(do, arrived, d, k):
        h = y if k == 0 else 1 - y

        def pass_on(block, right, left):
            if arrived:
                token_copy(CORE, block, h).wait_recv()
            if right:
                pl.when(z < planes - 1)(lambda: do(token_copy(RIGHT, block, h)))
            if left:
                pl.when(z > 0)(lambda: do(token_copy(LEFT, block, h)))
            if k == 0:
                do(token_copy(ACROSS, block, h))
            do(token_copy(CORE, block, h))

        if d == 0:
            pass_on(me, True, True)
        else:
            pl.when(z - d >= 0)(lambda: pass_on(ep_of(z - d, x, c), True, False))
            pl.when(z + d < planes)(lambda: pass_on(ep_of(z + d, x, c), False, True))

    def at_distance(d, act):
        if d == 0:
            act(z)
        else:
            pl.when(z - d >= 0)(lambda: act(z - d))
            pl.when(z + d < planes)(lambda: act(z + d))

    def token_moves(do, arrived):
        for step in range(planes + 2):
            if step < planes:
                for k in range(2):
                    on_line(do, arrived and step > 0, step, k)
            if 0 <= step - 1 < planes:

                def crossed(zz):
                    block = ep_of(zz, 1 - x, c)
                    if arrived:
                        token_copy(CORE, block, y).wait_recv()
                    do(token_copy(SIDE, block, y))
                    do(token_copy(CORE, block, y))

                at_distance(step - 1, crossed)
            if 0 <= step - 2 < planes:

                def sided(zz):
                    block = ep_of(zz, 1 - x, c)
                    if arrived:
                        token_copy(CORE, block, 1 - y).wait_recv()
                    do(token_copy(CORE, block, 1 - y))

                at_distance(step - 2, sided)

    token_moves(lambda copy: copy.start(), True)
    for zz in range(planes):
        for xx in range(2):
            for h in range(2):
                token_copy(CORE, ep_of(zz, xx, 1 - c), h).wait_recv()

    loads[0].wait()
    loads[1].wait()
    step_f = 256

    def project(i, carry):
        cols = pl.ds(pl.multiple_of(i * step_f, step_f), step_f)
        gate = jnp.dot(tok[:, :width], w_gate[:, cols], preferred_element_type=jnp.float32)
        upper = jnp.dot(tok[:, :width], w_up[:, cols], preferred_element_type=jnp.float32)
        value = (gate / (1.0 + jnp.exp(-gate)) * upper).astype(jnp.bfloat16)
        value = value.reshape(planes * 2, 2, rows, step_f)
        for cc in range(2):
            hid[cc, :, cols] = value[:, cc].reshape(planes * 2 * rows, step_f)
        return carry

    lax.fori_loop(0, hidden // step_f, project, 0)

    table = tok[:, width : width + LANES].astype(jnp.float32) + tok[:, width + LANES :].astype(
        jnp.float32
    )
    every = lax.broadcasted_iota(jnp.int32, table.shape, 1)
    chosen = jnp.sum(jnp.where(every == me, table, 0.0), axis=1, keepdims=True)
    chosen = jnp.broadcast_to(chosen, table.shape).reshape(planes * 2, 2, rows, LANES)
    for cc in range(2):
        wcol[cc] = chosen[:, cc].reshape(planes * 2 * rows, LANES)

    loads[2].wait()
    step_n = 512

    def expand(cc, dst):
        def one(i, carry):
            cols = pl.ds(pl.multiple_of(i * step_n, step_n), step_n)
            value = jnp.dot(hid[cc], w_down[:, cols], preferred_element_type=jnp.float32)
            value = value * wcol[cc][:, :1]
            for zz in range(planes):
                for xx in range(2):
                    for yy in range(2):
                        first = jnp.where(cc == 0, yy, xx)
                        second = jnp.where(cc == 0, xx, yy)
                        at = ((zz * 2 + xx) * 2 + yy) * sub
                        dst[zz, first, second, :, cols] = value[at : at + sub].astype(jnp.bfloat16)
            return carry

        lax.fori_loop(0, width // step_n, one, 0)

    def core_copy(t):
        return pltpu.make_async_remote_copy(
            src_ref=theirs.at[t], dst_ref=from_core.at[t],
            send_sem=core_send.at[t], recv_sem=core_recv.at[t],
            device_id=device(CORE), device_id_type=MESH,
        )

    expand(1 - c, theirs)
    for d in range(planes - 1, -1, -1):
        at_distance(d, lambda t: core_copy(t).start())
    expand(c, part)

    a = jnp.where(c == 0, y, x)
    b = jnp.where(c == 0, x, y)
    swap_y = (me, 1 - y)
    swap_x = (ep_of(z, 1 - x, c), y)
    first_device = tuple(jnp.where(c == 0, p, q) for p, q in zip(swap_y, swap_x))
    last_device = tuple(jnp.where(c == 0, q, p) for p, q in zip(swap_y, swap_x))

    def first_copy(t):
        return pltpu.make_async_remote_copy(
            src_ref=part.at[t, 1 - a], dst_ref=from_first.at[t],
            send_sem=first_send.at[t], recv_sem=first_recv.at[t],
            device_id=first_device, device_id_type=MESH,
        )

    def add_core(t):
        core_copy(t).wait_recv()
        part[t] = (part[t].astype(jnp.float32) + from_core[t].astype(jnp.float32)).astype(
            jnp.bfloat16
        )
        first_copy(t).start()

    for d in range(planes - 1, -1, -1):
        at_distance(d, add_core)

    def line_copy(side, t):
        return pltpu.make_async_remote_copy(
            src_ref=line_out.at[t], dst_ref=line_in.at[side, t],
            send_sem=line_send.at[t], recv_sem=line_recv.at[side, t],
            device_id=device(RIGHT if side == 0 else LEFT), device_id_type=MESH,
        )

    def kept(t):
        first_copy(t).wait_recv()
        return part[t, a].astype(jnp.float32) + from_first[t].astype(jnp.float32)

    def relay(side, t):
        line_out[t] = kept(t).astype(jnp.bfloat16)
        inner = z > 0 if side == 0 else z < planes - 1

        @pl.when(inner)
        def _():
            line_copy(side, t).wait_recv()
            line_out[t] = (
                line_out[t].astype(jnp.float32) + line_in[side, t].astype(jnp.float32)
            ).astype(jnp.bfloat16)

        line_copy(side, t).start()

    for d in range(planes - 1, 0, -1):
        pl.when(z + d < planes)(lambda: relay(0, z + d))
        pl.when(z - d >= 0)(lambda: relay(1, z - d))

    last_out[...] = kept(z)

    def gathered(side):
        line_copy(side, z).wait_recv()
        last_out[...] = last_out[...] + line_in[side, z].astype(jnp.float32)

    pl.when(z > 0)(lambda: gathered(0))
    pl.when(z < planes - 1)(lambda: gathered(1))
    line_out[z] = last_out[...].astype(jnp.bfloat16)
    final = pltpu.make_async_remote_copy(
        src_ref=line_out.at[z, 1 - b], dst_ref=last_in,
        send_sem=last_send, recv_sem=last_recv,
        device_id=last_device, device_id_type=MESH,
    )
    final.start()
    final.wait_recv()
    out_ref[...] = (last_out[b] + last_in[...].astype(jnp.float32)).astype(out_ref.dtype)

    final.wait_send()
    token_moves(lambda copy: copy.wait_send(), False)
    for t in range(planes):
        core_copy(t).wait_send()
        first_copy(t).wait_send()
    for d in range(1, planes):
        pl.when(z + d < planes)(lambda: line_copy(0, z + d).wait_send())
        pl.when(z - d >= 0)(lambda: line_copy(1, z - d).wait_send())


def by_gather(tokens, expert_ids, route_logits, expert_gate, expert_up, expert_down):
    rows, width = tokens.shape
    hidden = expert_gate.shape[2]
    n_ep, n_dp = lax.axis_size("ep"), lax.axis_size("dp")
    planes = n_ep // 4
    wide = width + 2 * LANES
    sub = rows // n_dp
    vmem = pl.BlockSpec(memory_space=pltpu.VMEM)
    anywhere = pl.BlockSpec(memory_space=pl.ANY)
    bf16, f32, dma = jnp.bfloat16, jnp.float32, pltpu.SemaphoreType.DMA
    return pl.pallas_call(
        functools.partial(exchange_kernel, planes),
        out_shape=jax.ShapeDtypeStruct((sub, width), bf16),
        in_specs=[vmem, vmem, vmem, anywhere, anywhere, anywhere],
        out_specs=vmem,
        scratch_shapes=[
            pltpu.VMEM((n_ep * rows, wide), bf16),
            pltpu.VMEM((width, hidden), bf16),
            pltpu.VMEM((width, hidden), bf16),
            pltpu.VMEM((hidden, width), bf16),
            pltpu.VMEM((2, n_ep * rows // 2, hidden), bf16),
            pltpu.VMEM((2, n_ep * rows // 2, LANES), f32),
            pltpu.VMEM((planes, 2, 2, sub, width), bf16),
            pltpu.VMEM((planes, 2, 2, sub, width), bf16),
            pltpu.VMEM((planes, 2, 2, sub, width), bf16),
            pltpu.VMEM((planes, 2, sub, width), bf16),
            pltpu.VMEM((planes, 2, sub, width), bf16),
            pltpu.VMEM((2, planes, 2, sub, width), bf16),
            pltpu.VMEM((2, sub, width), f32),
            pltpu.VMEM((sub, width), bf16),
            dma((3,)),
            dma((5, n_ep, 2)),
            dma((n_ep, 2)),
            dma((planes,)),
            dma((planes,)),
            dma((planes,)),
            dma((planes,)),
            dma((planes,)),
            dma((2, planes)),
            dma,
            dma,
        ],
        compiler_params=pltpu.CompilerParams(
            collective_id=0, has_side_effects=True, vmem_limit_bytes=56 * 1024 * 1024
        ),
    )(tokens, expert_ids, route_logits, expert_gate, expert_up, expert_down)


def on_device(tokens, expert_ids, route_logits, expert_gate, expert_up, expert_down):
    rows, width = tokens.shape
    n_ep, n_dp = lax.axis_size("ep"), lax.axis_size("dp")
    crowded = 4 * max(1, rows * expert_ids.shape[1] // n_ep) >= rows
    fits = n_dp == 2 and n_ep % 4 == 0 and n_ep <= LANES and rows == 16 and width % 512 == 0
    fits = fits and expert_gate.shape[0] == 1 and expert_gate.shape[2] % 256 == 0
    run = by_gather if crowded and fits else by_slots
    return run(tokens, expert_ids, route_logits, expert_gate, expert_up, expert_down)


def solution(mesh):
    placed = (
        P("ep", None),
        P("ep", None),
        P("ep", None),
        P("ep", None, "dp"),
        P("ep", None, "dp"),
        P("ep", "dp", None),
    )
    return jax.shard_map(
        on_device, mesh=mesh, in_specs=placed, out_specs=P(("ep", "dp"), None), check_vma=False
    )
```

profile of v0, /device:TPU:6, one launch (start us, length us, event | category | flops | bytes accessed | tf_op | source)
XLA Modules:
  0.0 402.3 jit_solution(13666367632085230634)
XLA Ops:
  6.5 0.9 copy.20
  7.4 0.1 eq.15
  7.5 0.1 reshape.87
  7.6 0.1 fusion.13
  7.7 0.2 reduce_window_sum.11
  7.9 0.2 select_reduce_fusion
  8.1 1.0 scatter_custom_fusion
  9.1 0.9 concatenate.3
  10.0 4.2 %gather_fusion = bf16[512,3584]{1,0:T(8,128)(2,1)} fusion(bf16[17,3584]{1,0:T(8,128)(2,1)S(1)} %concatenate.3, s32[1024]{0:T(1024)S(1)} %pad_clamp_fusion.1), kind=kCustom, calls=%fused_computation | custom fusion | bytes 7342080 | tf_op jit(solution)/shard_map/gather | solution.py:30
  14.2 7.0 %reshape.88 = bf16[128,4,3584]{2,1,0:T(4,128)(2,1)} reshape(bf16[512,3584]{1,0:T(8,128)(2,1)} %gather_fusion) | data formatting | bytes 7340032 | tf_op jit(solution)/shard_map/reshape | solution.py:30
  21.2 184.3 %all_to_all.10 = bf16[128,4,3584]{2,1,0:T(4,128)(2,1)} all-to-all(bf16[128,4,3584]{2,1,0:T(4,128)(2,1)} %reshape.88), channel_id=1, replica_groups=mesh['ep'=128,'dp'=4] {'ep'}, dimensions={0} | all-to-all | bytes 7340032 | tf_op jit(solution)/shard_map/all_to_all | solution.py:31
  205.5 6.7 %reshape.89 = bf16[512,3584]{1,0:T(8,128)(2,1)} reshape(bf16[128,4,3584]{2,1,0:T(4,128)(2,1)} %all_to_all.10) | data formatting | bytes 7340032 | tf_op jit(solution)/shard_map/reshape | solution.py:32
  212.2 3.9 fusion.4
  216.1 0.4 copy-done.3
  216.5 1.1 fusion.9
  217.7 2.9 convolution_convert_fusion
  220.7 47.2 %reduce-scatter.2.cloned.1.call-done = bf16[128,1,3584]{2,0,1:T(8,128)(2,1)} async-done(((bf16[128,4,3584]{2,0,1:T(8,128)(2,1)}), bf16[128,1,3584]{2,0,1:T(8,128)(2,1)}) %reduce-scatter.2.cloned.1.call-update) | async-done | bytes 917520 | tf_op jit(solution)/shard_map/reduce_scatter | solution.py:43
  267.8 0.5 broadcast.120
  268.3 2.5 reduce
  270.8 1.1 reshape.121
  271.9 17.0 %all-to-all-start.1 = ((bf16[128,2,1792]{2,1,0:T(2,128)(2,1)}), bf16[128,2,1792]{2,1,0:T(2,128)(2,1)S(1)}, u32[]{:S(2)}, u32[]{:S(2)}) async-start(bf16[128,2,1792]{2,1,0:T(2,128)(2,1)} %reshape.121), calls=%async_computation.2 | async-start | bytes 1835008 | tf_op jit(solution)/shard_map/all_to_all | solution.py:47
  289.0 0.1 and.14
  289.1 0.1 copy.21
  289.2 0.1 fusion.14
  289.4 48.0 %all-to-all-done.1 = bf16[128,2,1792]{2,1,0:T(2,128)(2,1)S(1)} async-done(((bf16[128,2,1792]{2,1,0:T(2,128)(2,1)}), bf16[128,2,1792]{2,1,0:T(2,128)(2,1)S(1)}, u32[]{:S(2)}, u32[]{:S(2)}) %all-to-all-start.1) | async-done | bytes 917536 | tf_op jit(solution)/shard_map/all_to_all | solution.py:47
  337.4 2.1 reshape.122
  339.5 1.6 copy.29
  341.1 2.0 gather_fusion.1
  343.2 2.5 fusion
  345.7 1.3 dynamic-slice
  347.7 46.3 %all-reduce.4.cloned.1.call-done = bf16[16,3584]{1,0:T(8,128)(2,1)} async-done(((bf16[16,3584]{1,0:T(8,128)(2,1)}), bf16[16,3584]{1,0:T(8,128)(2,1)}) %all-reduce.4.cloned.1.call-update) | async-done | bytes 114704
  394.0 1.4 constant_dynamic-slice_fusion
  (19 shorter events, 0.3 us)
Async XLA Ops:
  6.5 211.2 %copy-start = (bf16[1,256,3584]{2,1,0:T(8,128)(2,1)S(1)}, bf16[1,256,3584]{2,1,0:T(8,128)(2,1)}, u32[]{:S(2)}) copy-start(bf16[1,256,3584]{2,1,0:T(8,128)(2,1)} %param.11) | copy-start | bytes 5505028
  6.5 261.3 %reduce-scatter.2.cloned.1.call-start = ((), (), s32[]{:S(2)}) async-start(), calls=%async_computation.3 | async-start | bytes 4587520 | tf_op jit(solution)/shard_map/reduce_scatter | solution.py:43
  212.2 3.9 copy-start.1
  212.2 4.3 %copy-start.3 = (bf16[1,3584,256]{2,1,0:T(8,128)(2,1)S(1)}, bf16[1,3584,256]{2,1,0:T(8,128)(2,1)}, u32[]{:S(2)}) copy-start(bf16[1,3584,256]{2,1,0:T(8,128)(2,1)} %param.10) | copy-start | bytes 5505028
  220.6 68.5 %copy-start.2 = (f32[16,8]{0,1:T(8,128)S(1)}, f32[16,8]{0,1:T(8,128)}, u32[]{:S(2)}) copy-start(f32[16,8]{0,1:T(8,128)} %param.8) | copy-start | bytes 1540
  271.9 65.4 %all-to-all-start.1 = ((bf16[128,2,1792]{2,1,0:T(2,128)(2,1)}), bf16[128,2,1792]{2,1,0:T(2,128)(2,1)S(1)}, u32[]{:S(2)}, u32[]{:S(2)}) async-start(bf16[128,2,1792]{2,1,0:T(2,128)(2,1)} %reshape.121), calls=%async_computation.2 | async-start | bytes 1835008 | tf_op jit(solution)/shard_map/all_to_all | solution.py:47
  289.0 105.0 %all-reduce.4.cloned.1.call-start = ((), (), s32[]{:S(2)}) async-start(), calls=%async_computation.4 | async-start | bytes 229376
Sparse Core Ops, SparseCore 0:
  220.8 46.9 reduce-scatter.1
  345.9 48.0 all-reduce.3
where the time goes:
time: 403 us; the launch traced here: 402 us
  blocking collectives  184 us (46%)
  waiting for transfers between devices  141 us (35%)
  local copies, waits for them, and re-layouts  31.7 us (8%)
  starting transfers between devices  17.1 us (4%)
  between operations  14.2 us (4%)
  matrix products  7.89 us (2%)
  other arithmetic  5.68 us (1%)
    all_to_all x1, blocking collectives, by_slots(): lax.all_to_all(outgoing, 'ep', split_axis=0, concat_axis=0, tiled=True)  184 us
    all_to_all x1, waiting for transfers between devices, by_slots(): lax.all_to_all(reduced, 'ep', split_axis=0, concat_axis=0, tiled=True)  48 us
    reduce_scatter x1, waiting for transfers between devices, by_slots(): lax.psum_scatter(partial_value.astype(jnp.bfloat16), 'dp', scatter_dimens...  47.2 us
    unnamed x3, waiting for transfers between devices  46.4 us
    all_to_all x1, starting transfers between devices, by_slots(): lax.all_to_all(reduced, 'ep', split_axis=0, concat_axis=0, tiled=True)  17 us
    unnamed x15, local copies, waits for them, and re-layouts  8.91 us
  transfers between devices with their start and end apart: 3, of which 3 were waited for; matrix products, arithmetic and copies ran while one was open for 0% of the time, Pallas kernels for 0%

commit v1 on v0

v1 whole, which is shorter than its diff:
```python
import functools

import jax
import jax.numpy as jnp
from jax import lax
from jax.experimental import pallas as pl
from jax.experimental.pallas import tpu as pltpu
from jax.sharding import PartitionSpec as P

route_scale = 2.5


def by_slots(tokens, expert_ids, route_logits, expert_gate, expert_up, expert_down):
    tok_rows, width = tokens.shape
    top = expert_ids.shape[1]
    n_ep = lax.axis_size("ep")
    n_dp = lax.axis_size("dp")
    experts = n_ep
    capacity = min(tok_rows, 4 * max(1, tok_rows * top // experts))
    flat_ids = expert_ids.reshape(-1).astype(jnp.int32)
    onehot = (flat_ids[:, None] == jnp.arange(experts, dtype=jnp.int32)[None, :]).astype(jnp.int32)
    earlier = jnp.cumsum(onehot, axis=0).astype(jnp.int32) - onehot
    within = jnp.sum(earlier * onehot, axis=1).astype(jnp.int32)
    slot_index = flat_ids * capacity + within
    token_of_slot = jnp.arange(tok_rows * top, dtype=jnp.int32) // top
    source_row = (
        jnp.full((experts * capacity,), tok_rows, jnp.int32).at[slot_index].set(token_of_slot)
    )
    extended = jnp.concatenate([tokens, jnp.zeros((1, width), tokens.dtype)], axis=0)
    outgoing = extended[source_row].reshape(n_ep, capacity, width)
    arrived = lax.all_to_all(outgoing, "ep", split_axis=0, concat_axis=0, tiled=True)
    received = arrived.reshape(n_ep * capacity, width)
    gate = jnp.dot(received, expert_gate[0], preferred_element_type=jnp.float32)
    upper = jnp.dot(received, expert_up[0], preferred_element_type=jnp.float32)
    hidden = (jax.nn.silu(gate) * upper).astype(jnp.bfloat16)
    partial_value = jnp.dot(hidden, expert_down[0], preferred_element_type=jnp.float32)
    partial_value = partial_value.reshape(n_ep, capacity, width)
    scores = jax.nn.sigmoid(route_logits)
    weights = route_scale * scores / jnp.sum(scores, axis=1, keepdims=True)
    member = lax.axis_index("dp")
    quarter = capacity // n_dp
    reduced = (
        lax.psum_scatter(partial_value.astype(jnp.bfloat16), "dp", scatter_dimension=1, tiled=True)
        .astype(jnp.float32)
        .astype(jnp.bfloat16)
    )
    back = lax.all_to_all(reduced, "ep", split_axis=0, concat_axis=0, tiled=True)
    offset = within - member * quarter
    held = ((offset >= 0) & (offset < quarter)).astype(jnp.float32)
    picked = flat_ids * quarter + jnp.clip(offset, 0, quarter - 1)
    values = back.reshape(experts * quarter, width)[picked].reshape(tok_rows, top, width)
    masked = weights * held.reshape(tok_rows, top)
    contrib = jnp.sum(masked[:, :, None] * values.astype(jnp.float32), axis=1)
    routed = lax.psum_scatter(
        contrib.astype(jnp.bfloat16), "dp", scatter_dimension=0, tiled=True
    ).astype(jnp.float32)
    return routed.astype(jnp.bfloat16)


MESH = pl.DeviceIdType.MESH
LANES = 128
SLOTS = 4


def exchange_kernel(
    nx, nz, per, tokens_ref, ids_ref, logits_ref, gate_hbm, up_hbm, down_hbm, out_ref,
    w_gate, w_up, w_down, block, lift, sent, gathered, own, other, from_y, summed, back,
    local, line_out, line_in, last_out, last_in,
    weight_sem, z_send, z_recv, x_send, x_recv, y_send, y_recv, ry_send, ry_recv,
    rx_send, rx_recv, rz_send, rz_recv, last_send, last_recv,
):
    rows, width = tokens_ref.shape
    top = ids_ref.shape[1]
    half, quarter = width // 2, width // 4
    reach = nz // 2
    groups = nz // per
    tall = per * SLOTS
    wide = 2 * nx * tall
    me, y = lax.axis_index("ep"), lax.axis_index("dp")
    c, z, x = me % 2, (me // 2) % nz, me // (2 * nz)
    mine = y % 2
    seat = 2 * x + c

    def device(i, d, h, j):
        xx, zz, yy = (x + i + nx) % nx, (z + d + nz) % nz, (y + j + 4) % 4
        return ((xx * nz + zz) * 2 + (c + h) % 2, yy)

    def remote(src, dst, send, recv, to):
        return pltpu.make_async_remote_copy(
            src_ref=src, dst_ref=dst, send_sem=send, recv_sem=recv,
            device_id=to, device_id_type=MESH,
        )

    loads = [
        pltpu.make_async_copy(src.at[0], dst, weight_sem.at[i])
        for i, (src, dst) in enumerate(((gate_hbm, w_gate), (up_hbm, w_up), (down_hbm, w_down)))
    ]
    for load in loads:
        load.start()

    others = [(i, h) for i in range(nx) for h in range(2) if i or h]
    peers = [device(0, 1, 0, 0), device(0, -1, 0, 0)]
    peers += [device(i, 0, h, 0) for i, h in others]
    peers += [device(0, 0, 0, j) for j in (1, 2, 3)]
    barrier = pltpu.get_barrier_semaphore()
    for peer in peers:
        pl.semaphore_signal(barrier, inc=1, device_id=peer, device_id_type=MESH)

    def lanes_of(part, size):
        return pl.ds(pl.multiple_of(part * size, LANES), size)

    scores = jax.nn.sigmoid(logits_ref[...])
    weights = route_scale * scores / jnp.sum(scores, axis=1, keepdims=True)
    lane = lax.broadcasted_iota(jnp.int32, (rows, LANES), 1)
    dense = jnp.zeros((rows, LANES), jnp.float32)
    for k in range(top):
        dense = dense + jnp.where(lane == ids_ref[:, k : k + 1], weights[:, k : k + 1], 0.0)
    block[z, :, :half] = tokens_ref[:, lanes_of(mine, half)]
    block[z, :, half:] = dense.astype(jnp.bfloat16)

    span = per * rows
    column = lax.broadcasted_iota(jnp.int32, (LANES, wide), 1) // tall
    expert = ((column // 2) * nz + z) * 2 + column % 2
    chosen_by = (lax.broadcasted_iota(jnp.int32, (LANES, wide), 0) == expert).astype(jnp.bfloat16)
    first = lax.broadcasted_iota(jnp.int32, (span, span), 0)
    second = lax.broadcasted_iota(jnp.int32, (span, span), 1)
    before = ((first // rows == second // rows) & (second < first)).astype(jnp.bfloat16)
    slot = lax.broadcasted_iota(jnp.int32, (span, wide), 1) % tall
    at_row = lax.broadcasted_iota(jnp.int32, (span, wide), 0)
    in_block = slot // SLOTS == at_row // rows
    slot_rank = (slot % SLOTS).astype(jnp.float32)

    pl.semaphore_wait(barrier, len(peers))

    def z_copy(way, d):
        at = (z - d + 1 + nz) % nz if way == 0 else (z + d - 1) % nz
        to = device(0, 1 if way == 0 else -1, 0, 0)
        return remote(block.at[at], block.at[at], z_send.at[way, d], z_recv.at[way, d], to)

    def place(order):
        step = (order + 1) // 2
        return (jnp.where(order % 2 == 1, z - step, z + step) + nz) % nz

    def x_copy(k, i, h):
        to = 2 * ((x + i) % nx) + (c + h) % 2
        return remote(
            sent.at[k, to], gathered.at[k, seat, :, lanes_of(mine, half)],
            x_send.at[k, i, h], x_recv.at[k, i, h], device(i, 0, h, 0),
        )

    def y_copy(k, i, side):
        at = (x - i + nx) % nx
        ref = gathered.at[k, pl.ds(2 * at, 2), :, lanes_of(2 * mine + side, quarter)]
        to = device(0, 0, 0, 2 * side - 1)
        return remote(ref, ref, y_send.at[k, i, side], y_recv.at[k, i, side], to)

    def ry_copy(k, side):
        to = device(0, 0, 0, 2 * side - 1)
        return remote(
            other.at[k, side], from_y.at[k, side], ry_send.at[k, side], ry_recv.at[k, side], to
        )

    def rx_copy(k, i, h):
        to = 2 * ((x - i + nx) % nx) + (c + h) % 2
        return remote(
            summed.at[k, to], back.at[k, seat],
            rx_send.at[k, i, h], rx_recv.at[k, i, h], device(-i, 0, h, 0),
        )

    z_copy(0, 1).start()
    z_copy(1, 1).start()
    for load in loads:
        load.wait()

    def spread(k):
        def step(j, carry):
            d = (k * per) // 2 + 1 + j
            z_copy(0, d).wait_recv()
            pl.when(d < reach)(lambda: z_copy(0, d + 1).start())

            @pl.when(d < reach)
            def _():
                z_copy(1, d).wait_recv()
                pl.when(d < reach - 1)(lambda: z_copy(1, d + 1).start())

            return carry

        lax.fori_loop(0, per // 2, step, 0)
        places = [place(k * per + i) for i in range(per)]
        got = jnp.concatenate([block[at, :, :half] for at in places], axis=0)
        table = jnp.concatenate([block[at, :, half:] for at in places], axis=0)
        share = jnp.dot(table, chosen_by, preferred_element_type=jnp.float32)
        named = share > 0.0
        rank = jnp.dot(
            before, jnp.where(named, 1.0, 0.0).astype(jnp.bfloat16),
            preferred_element_type=jnp.float32,
        )
        hit = in_block & named & (rank == slot_rank)
        lift[k] = jnp.where(hit, share, 0.0).astype(jnp.bfloat16)
        take = jnp.where(hit, 1.0, 0.0).T.astype(jnp.bfloat16)
        value = jnp.dot(take, got, preferred_element_type=jnp.float32)
        sent[k] = value.astype(jnp.bfloat16).reshape(2 * nx, tall, half)
        for i, h in others:
            x_copy(k, i, h).start()
        gathered[k, seat, :, lanes_of(mine, half)] = sent[k, seat]

    def relay(k):
        for i in range(nx):
            for h in range(2):
                if i or h:
                    x_copy(k, i, h).wait_recv()
            for side in range(2):
                y_copy(k, i, side).start()

    def compute(k):
        for i in range(nx):
            for side in range(2):
                y_copy(k, i, side).wait_recv()
        value = gathered[k].reshape(wide, width)
        gate = jnp.dot(value, w_gate[...], preferred_element_type=jnp.float32)
        upper = jnp.dot(value, w_up[...], preferred_element_type=jnp.float32)
        hidden = (gate / (1.0 + jnp.exp(-gate)) * upper).astype(jnp.bfloat16)

        def down(part):
            value = jnp.dot(
                hidden, w_down[:, lanes_of(part, quarter)], preferred_element_type=jnp.float32
            )
            return value.reshape(2 * nx, tall, quarter)

        for side in range(2):
            other[k, side] = down(2 * (1 - mine) + side).astype(jnp.bfloat16)
            ry_copy(k, side).start()
        for side in range(2):
            own[k, side] = down(2 * mine + side)

    def reduce(k):
        for side in range(2):
            ry_copy(k, side).wait_recv()
            summed[k, :, :, side * quarter : (side + 1) * quarter] = (
                own[k, side] + from_y[k, side].astype(jnp.float32)
            ).astype(jnp.bfloat16)
        for i, h in others:
            rx_copy(k, i, h).start()
        back[k, seat] = summed[k, seat]

    def combine(k):
        for i, h in others:
            rx_copy(k, i, h).wait_recv()
        value = jnp.dot(
            lift[k], back[k].reshape(wide, half), preferred_element_type=jnp.float32
        )
        local[pl.ds(k * per, per)] = value.reshape(per, rows, half)

    stages = (spread, relay, compute, reduce, combine)

    def tick(t, carry):
        for lag, stage in enumerate(stages):
            pl.when((t >= lag) & (t - lag < groups))(functools.partial(stage, t - lag))
        return carry

    lax.fori_loop(0, groups + len(stages) - 1, tick, 0)

    def rz_copy(way, d):
        to = device(0, 1 if way == 0 else -1, 0, 0)
        return remote(
            line_out.at[way, d], line_in.at[way, d], rz_send.at[way, d], rz_recv.at[way, d], to
        )

    farthest = (reach - 1, reach)

    def homeward(way, d):
        value = local[2 * d if way == 0 else 2 * d - 1]
        if d < farthest[way]:
            rz_copy(way, d + 1).wait_recv()
            value = value + line_in[way, d + 1].astype(jnp.float32)
        line_out[way, d] = value.astype(jnp.bfloat16)
        rz_copy(way, d).start()

    for d in range(reach, 0, -1):
        for way in (1, 0):
            if d <= farthest[way]:
                homeward(way, d)
    value = local[0]
    for way in range(2):
        rz_copy(way, 1).wait_recv()
        value = value + line_in[way, 1].astype(jnp.float32)
    last_out[...] = value.reshape(4, rows // 4, half)

    def last_copy(j):
        return remote(
            last_out.at[(y + j) % 4], last_in.at[y], last_send.at[j], last_recv.at[j],
            device(0, 0, 0, j),
        )

    for j in (2, 1, 3):
        last_copy(j).start()
    last_in[y] = last_out[y]
    for j in (1, 3, 2):
        last_copy(j).wait_recv()
    for side in range(2):
        out_ref[:, side * half : (side + 1) * half] = (
            last_in[side] + last_in[side + 2]
        ).astype(out_ref.dtype)

    for d in range(1, reach + 1):
        for way in range(2):
            if d <= (reach, reach - 1)[way]:
                z_copy(way, d).wait_send()
            if d <= farthest[way]:
                rz_copy(way, d).wait_send()
    for j in (1, 2, 3):
        last_copy(j).wait_send()

    def drain(k, carry):
        for i, h in others:
            x_copy(k, i, h).wait_send()
            rx_copy(k, i, h).wait_send()
        for side in range(2):
            for i in range(nx):
                y_copy(k, i, side).wait_send()
            ry_copy(k, side).wait_send()
        return carry

    lax.fori_loop(0, groups, drain, 0)


def by_exchange(tokens, expert_ids, route_logits, expert_gate, expert_up, expert_down):
    rows, width = tokens.shape
    hidden = expert_gate.shape[2]
    nx = 4
    nz = lax.axis_size("ep") // (2 * nx)
    per = 4
    groups, tall, reach = nz // per, per * SLOTS, nz // 2
    wide = 2 * nx * tall
    half, quarter, sub = width // 2, width // 4, rows // 4
    vmem = pl.BlockSpec(memory_space=pltpu.VMEM)
    anywhere = pl.BlockSpec(memory_space=pl.ANY)
    bf16, f32, dma = jnp.bfloat16, jnp.float32, pltpu.SemaphoreType.DMA
    return pl.pallas_call(
        functools.partial(exchange_kernel, nx, nz, per),
        out_shape=jax.ShapeDtypeStruct((sub, width), bf16),
        in_specs=[vmem, vmem, vmem, anywhere, anywhere, anywhere],
        out_specs=vmem,
        scratch_shapes=[
            pltpu.VMEM((width, hidden), bf16),
            pltpu.VMEM((width, hidden), bf16),
            pltpu.VMEM((hidden, width), bf16),
            pltpu.VMEM((nz, rows, half + LANES), bf16),
            pltpu.VMEM((groups, per * rows, wide), bf16),
            pltpu.VMEM((groups, 2 * nx, tall, half), bf16),
            pltpu.VMEM((groups, 2 * nx, tall, width), bf16),
            pltpu.VMEM((groups, 2, 2 * nx, tall, quarter), f32),
            pltpu.VMEM((groups, 2, 2 * nx, tall, quarter), bf16),
            pltpu.VMEM((groups, 2, 2 * nx, tall, quarter), bf16),
            pltpu.VMEM((groups, 2 * nx, tall, half), bf16),
            pltpu.VMEM((groups, 2 * nx, tall, half), bf16),
            pltpu.VMEM((nz, rows, half), f32),
            pltpu.VMEM((2, reach + 1, rows, half), bf16),
            pltpu.VMEM((2, reach + 1, rows, half), bf16),
            pltpu.VMEM((4, sub, half), f32),
            pltpu.VMEM((4, sub, half), f32),
            dma((3,)),
            dma((2, reach + 1)),
            dma((2, reach + 1)),
            dma((groups, nx, 2)),
            dma((groups, nx, 2)),
            dma((groups, nx, 2)),
            dma((groups, nx, 2)),
            dma((groups, 2)),
            dma((groups, 2)),
            dma((groups, nx, 2)),
            dma((groups, nx, 2)),
            dma((2, reach + 1)),
            dma((2, reach + 1)),
            dma((4,)),
            dma((4,)),
        ],
        compiler_params=pltpu.CompilerParams(
            collective_id=0, has_side_effects=True, vmem_limit_bytes=56 * 1024 * 1024
        ),
    )(tokens, expert_ids, route_logits, expert_gate, expert_up, expert_down)


def on_device(tokens, expert_ids, route_logits, expert_gate, expert_up, expert_down):
    rows, width = tokens.shape
    n_ep, n_dp = lax.axis_size("ep"), lax.axis_size("dp")
    fits = n_dp == 4 and n_ep == LANES and rows == 16 and width % 512 == 0
    fits = fits and expert_gate.shape[0] == 1 and expert_gate.shape[2] % LANES == 0
    run = by_exchange if fits else by_slots
    return run(tokens, expert_ids, route_logits, expert_gate, expert_up, expert_down)


def solution(mesh):
    placed = (
        P("ep", None),
        P("ep", None),
        P("ep", None),
        P("ep", None, "dp"),
        P("ep", None, "dp"),
        P("ep", "dp", None),
    )
    return jax.shard_map(
        on_device, mesh=mesh, in_specs=placed, out_specs=P(("ep", "dp"), None), check_vma=False
    )
```

time: 403 us -> 119 us (0.30)
  blocking collectives: 184 us -> 0 us
  waiting for transfers between devices: 141 us -> 0 us
  Pallas kernels: 0 us -> 114 us
  local copies, waits for them, and re-layouts: 31.7 us -> 4.07 us
  starting transfers between devices: 17.1 us -> 0 us
  between operations: 14.2 us -> 0.01 us
  matrix products: 7.89 us -> 0 us
  other arithmetic: 5.68 us -> 0 us
    all_to_all x1 -> x0, blocking collectives: 184 us -> none  [by_slots(): lax.all_to_all(outgoing, 'ep', split_axis=0, concat_axis=0, tiled=True)]
    pallas_call x0 -> x1, Pallas kernels: none -> 114 us  [by_exchange(): pl.pallas_call(functools.partial(exchange_kernel, nx, nz, per), out_shape...]
    all_to_all x1 -> x0, waiting for transfers between devices: 48 us -> none  [by_slots(): lax.all_to_all(reduced, 'ep', split_axis=0, concat_axis=0, tiled=True)]
    reduce_scatter x1 -> x0, waiting for transfers between devices: 47.2 us -> none  [by_slots(): lax.psum_scatter(partial_value.astype(jnp.bfloat16), 'dp', scatter_dimens...]
    unnamed x3 -> x0, waiting for transfers between devices: 46.4 us -> none
    all_to_all x1 -> x0, starting transfers between devices: 17 us -> none  [by_slots(): lax.all_to_all(reduced, 'ep', split_axis=0, concat_axis=0, tiled=True)]
    reshape x3 -> x0, local copies, waits for them, and re-layouts: 13.8 us -> none  [the longest x1 7 us: by_slots(): outgoing = extended[source_row].reshape(n_ep, capacity, width)]
    dot_general x3 -> x0, matrix products: 7.89 us -> none  [the longest x1 3.86 us: by_slots(): gate = jnp.dot(received, expert_gate[0], preferred_element_type=jnp.float32)]
  transfers between devices with their start and end apart: 3 -> 0, of which waited for: 3 -> 0; matrix products, arithmetic and copies ran while one was open for 0% -> 0% of each run, Pallas kernels for 0% -> 0%
where the time goes in v1:
time: 119 us; the launch traced here: 118 us
  Pallas kernels  114 us (96%)
  local copies, waits for them, and re-layouts  4.07 us (3%)
    pallas_call x1, Pallas kernels, by_exchange(): pl.pallas_call(functools.partial(exchange_kernel, nx, nz, per), out_shape...  114 us
    unnamed x3, local copies, waits for them, and re-layouts  4.07 us

profile of v1, /device:TPU:6, one launch (start us, length us, event | category | flops | bytes accessed | tf_op | source)
XLA Modules:
  0.0 118.3 jit_solution(9194247510153436372)
XLA Ops:
  0.0 1.4 %copy.7.ids_ref = s32[16,8]{1,0:T(8,128)} copy(s32[16,8]{0,1:T(8,128)} %param.7) | data formatting | bytes 1024 | tf_op args[1]
  1.4 1.3 %copy.8.logits_ref = f32[16,8]{1,0:T(8,128)} copy(f32[16,8]{0,1:T(8,128)} %param.8) | data formatting | bytes 1024 | tf_op args[2]
  2.7 114.2 %shard_map.64 = bf16[4,3584]{1,0:T(4,128)(2,1)} custom-call(bf16[16,3584]{1,0:T(8,128)(2,1)} %tokens_ref.1, s32[16,8]{1,0:T(8,128)} %copy.7.ids_ref, f32[16,8]{1,0:T(8,128)} %copy.8.logits_ref, bf16[1,3584,256]{2,1,0:T(8,128)(2,1)} %gate_hbm.1, bf16[1,3584,256]{2,1,0:T(8,128)(2,1)} %up_hbm.1, bf16[1,256,3584]{2,1,0:T(8,128)(2,1)} %down_hbm.1), custom_call_target="tpu_custom_call" | custom-call | tf_op jit(solution)/shard_map/pallas_call | solution.py:339
  116.9 1.4 %copy.10 = bf16[4,3584]{1,0:T(4,128)(2,1)} copy(bf16[4,3584]{1,0:T(4,128)(2,1)} %shard_map.64) | data formatting | bytes 57344
